TPU v7x, 128 devices: a whole 4x4x4 slice. The times are simulated.
128 devices in a mesh: seq: 16 (over z, x), tp: 8 (over y, core).
Axes of the slice: x: 4, y: 4, z: 4, core: 2. Of those that a mesh axis runs over, the one named last changes fastest.
Arguments:
- tokens: bfloat16 [2048, 6144], P('seq', 'tp'), may hold values from -6 to 6
- router_weight: bfloat16 [6144, 8], P('tp'), may hold values from -0.15625 to 0.15625
- expert_ids: int32 [2048, 2], P('seq'), may hold values from 0 to 7, all different within a row; in each aligned block of 128 rows (0 to 127, 128 to 255, ...) at most 56 rows name the same one
- gate_weight: bfloat16 [16, 6144, 4096], P('seq', None, 'tp'), may hold values from -0.078125 to 0.078125
- up_weight: bfloat16 [16, 6144, 4096], P('seq', None, 'tp'), may hold values from -0.078125 to 0.078125
- down_weight: bfloat16 [16, 4096, 6144], P('seq', 'tp'), may hold values from -0.0625 to 0.0625
Outputs:
- mixed: bfloat16 [2048, 6144], P('seq', 'tp')
Inputs may be any that keep to these rules, and one draw needn't show every extreme that they name: `expert_ids`: each row names 2 different experts. In each aligned block of 128 rows (the tokens of one sequence group) no expert is named more than 56 times, a bound that some block reaches.
All inputs are finite; a program needn't handle non-finite values.
Results may differ from a plain program's by a relative error of at most 0.014.
Values may be sent and summed in bfloat16 or wider, within the bound.
No kernel may reach another device: no remote copies, remote signals or barrier semaphores. Data moves between devices by JAX's collectives and lax.ppermute only.
A program may use at most 128 MiB of HBM per device.

v0:
```python
import jax
import jax.numpy as jnp
from jax import lax
from jax.sharding import PartitionSpec as P

D = 6144
CAP = 56


def sent_to_all(array, axis):
    length = lax.axis_size(axis)
    return lax.all_to_all(
        jnp.broadcast_to(array[None], (length, *array.shape)), axis, 0, 0, tiled=True
    )


def over_copies(array, axis):
    return sent_to_all(array, axis).sum(axis=0)


def slot_numbers(expert_ids, experts):
    flat_ids = expert_ids.reshape(-1)
    onehot = (flat_ids[:, None] == jnp.arange(experts, dtype=jnp.int32)[None, :]).astype(jnp.int32)
    before = jnp.cumsum(onehot, axis=0) - onehot
    return (flat_ids, jnp.sum(before * onehot, axis=1))


def per_device(tokens, router_weight, expert_ids, gate_weight, up_weight, down_weight):
    seq_count = lax.axis_size("seq")
    experts = router_weight.shape[1]
    halves = seq_count // experts
    tok_rows, top_count = expert_ids.shape
    capacity = CAP
    width = D
    gate_slab = gate_weight[0]
    up_slab = up_weight[0]
    down_slab = down_weight[0]
    partial_logits = jnp.dot(tokens, router_weight, preferred_element_type=jnp.float32)
    logits = over_copies(partial_logits, "tp")
    chosen = expert_ids[:, :, None] == jnp.arange(experts, dtype=jnp.int32)[None, None, :]
    picked = jnp.sum(jnp.where(chosen, logits[:, None, :], 0.0), axis=2)
    gates = jax.nn.sigmoid(picked - picked[:, ::-1])
    flat_ids, slots = slot_numbers(expert_ids, experts)
    row_index = jnp.arange(seq_count * capacity, dtype=jnp.int32)
    row_expert = row_index // capacity // halves
    row_slot = row_index % capacity
    matches = (row_expert[:, None] == flat_ids[None, :]) & (row_slot[:, None] == slots[None, :])
    select = jnp.any(matches.reshape(seq_count * capacity, tok_rows, top_count), axis=2).astype(
        jnp.bfloat16
    )
    outgoing = jnp.dot(select, tokens, preferred_element_type=jnp.float32).astype(jnp.bfloat16)
    outgoing = outgoing.reshape(seq_count, capacity, tokens.shape[1])
    received = lax.all_to_all(outgoing, "seq", split_axis=0, concat_axis=0, tiled=True)
    count = received.shape[1]
    piece = lax.all_gather(received, "tp", axis=2, tiled=True)
    piece_rows = piece.reshape(-1, piece.shape[2])
    gate = jnp.dot(piece_rows, gate_slab, preferred_element_type=jnp.float32)
    up = jnp.dot(piece_rows, up_slab, preferred_element_type=jnp.float32)
    hidden = (jax.nn.silu(gate) * up).astype(jnp.bfloat16)
    partial_value = jnp.dot(hidden, down_slab, preferred_element_type=jnp.float32).reshape(
        seq_count, count, width
    )
    reduced = lax.psum_scatter(
        partial_value.astype(jnp.bfloat16), "tp", scatter_dimension=2, tiled=True
    ).astype(jnp.float32)
    returned = lax.all_to_all(
        reduced.astype(jnp.bfloat16), "seq", split_axis=0, concat_axis=0, tiled=True
    ).astype(reduced.dtype)
    columns = returned.shape[2]
    summed = jnp.sum(returned.reshape(experts, halves, capacity, columns), axis=1)
    summed = summed.reshape(experts * capacity, columns)
    gathered = summed[flat_ids * capacity + slots].reshape(tok_rows, top_count, columns)
    mixed = jnp.sum(gathered * gates[:, :, None], axis=1)
    return mixed.astype(jnp.bfloat16)


def solution(mesh):
    in_specs = (
        P("seq", "tp"),
        P("tp", None),
        P("seq", None),
        P("seq", None, "tp"),
        P("seq", None, "tp"),
        P("seq", "tp", None),
    )
    out_specs = P("seq", "tp")
    return jax.shard_map(
        per_device, mesh=mesh, in_specs=in_specs, out_specs=out_specs, check_vma=False
    )
```

profile of v0, /device:TPU:9, one launch (start us, length us, event | category | flops | bytes accessed | tf_op | source)
XLA Modules:
  0.0 233.1 jit_solution(17153037409730043633)
XLA Ops:
  6.5 0.0 copy-start
  6.5 0.8 copy.27
  7.4 0.1 eq.78
  7.5 0.1 eq.74
  7.7 0.6 reduce-window.6
  8.3 0.2 slice_reduce_fusion
  8.5 0.1 fusion.8
  8.6 0.1 eq.82
  8.8 0.1 copy.29
  8.8 1.0 and_reduce_fusion
  9.9 0.5 convolution_convert_fusion.1
  10.4 27.4 %all_to_all.15 = bf16[16,56,768]{2,1,0:T(8,128)(2,1)} all-to-all(bf16[16,56,768]{2,1,0:T(8,128)(2,1)S(1)} %bitcast.37), channel_id=1, replica_groups=mesh['seq'=16,'tp'=8] {'seq'}, dimensions={0} | all-to-all | bytes 2752512 | tf_op jit(solution)/shard_map/all_to_all | solution.py:53
  37.8 0.0 all-gather.2.cloned.1.call-update
  37.8 0.0 reduce-scatter.2.cloned.1.call-start
  37.8 59.0 %all-gather.2.cloned.1.call-done = bf16[16,56,6144]{2,1,0:T(8,128)(2,1)} async-done(((bf16[16,56,768]{2,1,0:T(8,128)(2,1)}), bf16[16,56,6144]{2,1,0:T(8,128)(2,1)}) %all-gather.2.cloned.1.call-update) | async-done | bytes 11010064 | tf_op jit(solution)/shard_map/all_gather | solution.py:55
  96.9 10.6 %fusion.3 = f32[896,512]{1,0:T(8,128)S(1)} fusion(bf16[896,6144]{1,0:T(8,128)(2,1)} %bitcast.40, bf16[1,6144,512]{2,1,0:T(8,128)(2,1)} %param.9), kind=kOutput, calls=%fused_computation.5 | convolution fusion | flops 5637144576 | bytes 19136512 | tf_op jit(solution)/shard_map/dot_general | solution.py:57
  107.5 8.0 %multiply_convert_fusion = bf16[896,512]{1,0:T(8,128)(2,1)S(1)} fusion(f32[896,512]{1,0:T(8,128)S(1)} %fusion.3, bf16[896,6144]{1,0:T(8,128)(2,1)S(1)} %bitcast.41, bf16[1,6144,512]{2,1,0:T(8,128)(2,1)} %param.10), kind=kOutput, calls=%fused_computation.8 | convolution fusion | flops 5639897088 | bytes 20054016 | tf_op jit(solution)/shard_map/dot_general | solution.py:58
  115.5 11.3 %convolution_convert_fusion = bf16[16,56,6144]{2,1,0:T(8,128)(2,1)} fusion(bf16[16,56,512]{2,1,0:T(8,128)(2,1)S(1)} %bitcast.42, bf16[1,512,6144]{2,1,0:T(8,128)(2,1)} %param.11), kind=kOutput, calls=%fused_computation.1 | convolution fusion | flops 5642649600 | bytes 18219008 | tf_op jit(solution)/shard_map/dot_general | solution.py:60
  126.8 0.0 reduce-scatter.2.cloned.1.call-update
  126.9 0.7 copy-done.2
  127.5 0.1 fusion.19
  127.7 7.9 %all_to_all.16 = f32[8,128,8]{1,2,0:T(8,128)S(1)} all-to-all(f32[8,128,8]{1,2,0:T(8,128)S(1)} %broadcast_in_dim.10), channel_id=1, replica_groups=mesh['seq'=16,'tp'=8] {'tp'}, dimensions={0} | all-to-all | bytes 65536 | tf_op jit(solution)/shard_map/all_to_all | solution.py:12
  135.6 56.1 %reduce-scatter.2.cloned.1.call-done = bf16[16,56,768]{2,1,0:T(8,128)(2,1)} async-done(((bf16[16,56,6144]{2,1,0:T(8,128)(2,1)}), bf16[16,56,768]{2,1,0:T(8,128)(2,1)}) %reduce-scatter.2.cloned.1.call-update) | async-done | bytes 1376272 | tf_op jit(solution)/shard_map/reduce_scatter | solution.py:63
  191.7 6.7 %all-to-all-start.1 = ((bf16[16,56,768]{2,1,0:T(8,128)(2,1)}), bf16[16,56,768]{2,1,0:T(8,128)(2,1)S(1)}, u32[]{:S(2)}, u32[]{:S(2)}) async-start(bf16[16,56,768]{2,1,0:T(8,128)(2,1)} %reduce-scatter.2.cloned.1.call-done), calls=%async_computation.2 | async-start | bytes 2752512 | tf_op jit(solution)/shard_map/all_to_all | solution.py:66
  198.4 0.1 copy.30
  198.5 0.1 mul.39
  198.7 0.1 copy.31
  198.8 24.0 %all-to-all-done.1 = bf16[16,56,768]{2,1,0:T(8,128)(2,1)S(1)} async-done(((bf16[16,56,768]{2,1,0:T(8,128)(2,1)}), bf16[16,56,768]{2,1,0:T(8,128)(2,1)S(1)}, u32[]{:S(2)}, u32[]{:S(2)}) %all-to-all-start.1) | async-done | bytes 1376288 | tf_op jit(solution)/shard_map/all_to_all | solution.py:66
  222.8 0.2 convert_reduce_fusion
  223.0 1.1 gather_fusion
  224.1 0.5 reshape.133
  224.6 1.7 multiply_reduce_fusion
  (19 shorter events, 0.2 us)
Async XLA Ops:
  6.5 3.3 %copy-start = (bf16[128,768]{1,0:T(8,128)(2,1)S(1)}, bf16[128,768]{1,0:T(8,128)(2,1)}, u32[]{:S(2)}) copy-start(bf16[128,768]{1,0:T(8,128)(2,1)} %param.6) | copy-start | bytes 589828
  6.5 90.3 %all-gather.2.cloned.1.call-start = ((), (), s32[]{:S(2)}) async-start(), calls=%async_computation.4 | async-start | bytes 12386304 | tf_op jit(solution)/shard_map/all_gather | solution.py:55
  37.8 153.9 %reduce-scatter.2.cloned.1.call-start = ((), (), s32[]{:S(2)}) async-start(), calls=%async_computation.5 | async-start | bytes 12386304 | tf_op jit(solution)/shard_map/reduce_scatter | solution.py:63
  96.9 10.6 %copy-start.3 = (bf16[16,56,6144]{2,1,0:T(8,128)(2,1)S(1)}, bf16[16,56,6144]{2,1,0:T(8,128)(2,1)}, u32[]{:S(2)}) copy-start(bf16[16,56,6144]{2,1,0:T(8,128)(2,1)} %all-gather.2.cloned.1.call-done) | copy-start | bytes 33030148
  126.8 0.7 copy-start.2
  126.8 71.5 %copy-start.1 = (s32[128,2]{0,1:T(2,128)S(1)}, s32[128,2]{0,1:T(2,128)}, u32[]{:S(2)}) copy-start(s32[128,2]{0,1:T(2,128)} %param.8) | copy-start | bytes 3076
  191.7 31.1 %all-to-all-start.1 = ((bf16[16,56,768]{2,1,0:T(8,128)(2,1)}), bf16[16,56,768]{2,1,0:T(8,128)(2,1)S(1)}, u32[]{:S(2)}, u32[]{:S(2)}) async-start(bf16[16,56,768]{2,1,0:T(8,128)(2,1)} %reduce-scatter.2.cloned.1.call-done), calls=%async_computation.2 | async-start | bytes 2752512 | tf_op jit(solution)/shard_map/all_to_all | solution.py:66
Sparse Core Ops, SparseCore 0:
  37.9 58.9 all-gather.1
  127.0 64.6 reduce-scatter.1
where the time goes:
time: 233 us
  waiting for transfers between devices  139 us (60%)
  blocking collectives  35.3 us (15%)
  matrix products  30.6 us (13%)
  between operations  13.6 us (6%)
  starting transfers between devices  6.71 us (3%)
  local copies, waits for them, and re-layouts  4.17 us (2%)
  other arithmetic  3.74 us (2%)
    all_gather x1, waiting for transfers between devices, per_device(): piece = lax.all_gather(received, 'tp', axis=2, tiled=True)  59 us
    reduce_scatter x1, waiting for transfers between devices, per_device(): lax.psum_scatter(partial_value.astype(jnp.bfloat16), 'tp', scatter_dimens...  56.1 us
    all_to_all x1, blocking collectives, per_device(): lax.all_to_all(outgoing, 'seq', split_axis=0, concat_axis=0, tiled=True)  27.4 us
    all_to_all x1, waiting for transfers between devices, per_device(): lax.all_to_all(reduced.astype(jnp.bfloat16), 'seq', split_axis=0, concat_...  24 us
    dot_general x1, matrix products, per_device(): jnp.dot(hidden, down_slab, preferred_element_type=jnp.float32)  11.3 us
    dot_general x1, matrix products, per_device(): gate = jnp.dot(piece_rows, gate_slab, preferred_element_type=jnp.float32)  10.6 us
    dot_general x1, matrix products, per_device(): up = jnp.dot(piece_rows, up_slab, preferred_element_type=jnp.float32)  8.03 us
    all_to_all x1, blocking collectives, sent_to_all(): lax.all_to_all(jnp.broadcast_to(array[None], (length, *array.shape)), axi...  7.9 us
  transfers between devices with their start and end apart: 3, of which 3 were waited for; matrix products, arithmetic and copies ran while one was open for 0% of the time, Pallas kernels for 0%

commit v1 on v0

--- a/solution.py
+++ b/solution.py
@@ -52,7 +52,9 @@
     outgoing = outgoing.reshape(seq_count, capacity, tokens.shape[1])
     received = lax.all_to_all(outgoing, "seq", split_axis=0, concat_axis=0, tiled=True)
     count = received.shape[1]
-    piece = lax.all_gather(received, "tp", axis=2, tiled=True)
+    piece = jnp.concatenate(
+        lax.all_to_all(jnp.stack([received] * lax.axis_size("tp")), "tp", 0, 0), axis=2
+    )
     piece_rows = piece.reshape(-1, piece.shape[2])
     gate = jnp.dot(piece_rows, gate_slab, preferred_element_type=jnp.float32)
     up = jnp.dot(piece_rows, up_slab, preferred_element_type=jnp.float32)

time: 233 us -> 324 us (1.39)
  blocking collectives: 35.3 us -> 163 us
  waiting for transfers between devices: 139 us -> 76.3 us
  local copies, waits for them, and re-layouts: 4.17 us -> 34.7 us
  matrix products: 30.6 us -> 25.8 us
    all_to_all x0 -> x1, blocking collectives: none -> 128 us  [per_device(): lax.all_to_all(jnp.stack([received] * lax.axis_size('tp')), 'tp', 0, 0)]
    all_gather x1 -> x0, waiting for transfers between devices: 59 us -> none  [per_device(): piece = lax.all_gather(received, 'tp', axis=2, tiled=True)]
    reshape x0 -> x1, local copies, waits for them, and re-layouts: none -> 22.3 us  [per_device(): jnp.concatenate(lax.all_to_all(jnp.stack([received] * lax.axis_size('tp')...]
    another operation x1 -> x2, local copies, waits for them, and re-layouts: 0.01 us -> 4.92 us  [the longest x1 4.92 us: per_device(): jnp.stack([received] * lax.axis_size('tp'))]
    dot_general x1, matrix products: 10.6 us -> 5.83 us  [per_device(): gate = jnp.dot(piece_rows, gate_slab, preferred_element_type=jnp.float32)]
    reduce_scatter x1, waiting for transfers between devices: 56.1 us -> 52.3 us  [per_device(): lax.psum_scatter(partial_value.astype(jnp.bfloat16), 'tp', scatter_dimens...]
    unnamed x9 -> x12, local copies, waits for them, and re-layouts: 1.52 us -> 4.77 us
  transfers between devices with their start and end apart: 3 -> 2, of which waited for: 3 -> 2; matrix products, arithmetic and copies ran while one was open for 0% -> 0% of each run, Pallas kernels for 0% -> 0%
where the time goes in v1:
time: 324 us
  blocking collectives  163 us (50%)
  waiting for transfers between devices  76.3 us (24%)
  local copies, waits for them, and re-layouts  34.7 us (11%)
  matrix products  25.8 us (8%)
  between operations  13.6 us (4%)
  starting transfers between devices  6.6 us (2%)
  other arithmetic  3.74 us (1%)
    all_to_all x1, blocking collectives, per_device(): lax.all_to_all(jnp.stack([received] * lax.axis_size('tp')), 'tp', 0, 0)  128 us
    reduce_scatter x1, waiting for transfers between devices, per_device(): lax.psum_scatter(partial_value.astype(jnp.bfloat16), 'tp', scatter_dimens...  52.3 us
    all_to_all x1, blocking collectives, per_device(): lax.all_to_all(outgoing, 'seq', split_axis=0, concat_axis=0, tiled=True)  27.2 us
    all_to_all x1, waiting for transfers between devices, per_device(): lax.all_to_all(reduced.astype(jnp.bfloat16), 'seq', split_axis=0, concat_...  24 us
    reshape x1, local copies, waits for them, and re-layouts, per_device(): jnp.concatenate(lax.all_to_all(jnp.stack([received] * lax.axis_size('tp')...  22.3 us
    dot_general x1, matrix products, per_device(): jnp.dot(hidden, down_slab, preferred_element_type=jnp.float32)  11.3 us
    dot_general x1, matrix products, per_device(): up = jnp.dot(piece_rows, up_slab, preferred_element_type=jnp.float32)  8.03 us
    all_to_all x1, blocking collectives, sent_to_all(): lax.all_to_all(jnp.broadcast_to(array[None], (length, *array.shape)), axi...  7.59 us
  transfers between devices with their start and end apart: 2, of which 2 were waited for; matrix products, arithmetic and copies ran while one was open for 0% of the time, Pallas kernels for 0%

profile of v1, /device:TPU:9, one launch (start us, length us, event | category | flops | bytes accessed | tf_op | source)
XLA Modules:
  0.0 324.0 jit_solution(17496300164440277337)
XLA Ops:
  6.5 0.8 copy.29
  7.4 0.1 eq.78
  7.5 0.1 eq.74
  7.7 0.6 reduce-window.6
  8.3 0.2 slice_reduce_fusion
  8.5 0.1 fusion.8
  8.6 0.1 eq.82
  8.8 0.1 copy.31
  8.8 1.0 and_reduce_fusion
  9.9 0.5 convolution_convert_fusion.1
  10.4 27.2 %all_to_all.20 = bf16[16,56,768]{2,1,0:T(8,128)(2,1)S(1)} all-to-all(bf16[16,56,768]{2,1,0:T(8,128)(2,1)S(1)} %bitcast.44), channel_id=1, replica_groups=mesh['seq'=16,'tp'=8] {'seq'}, dimensions={0} | all-to-all | bytes 2752512 | tf_op jit(solution)/shard_map/all_to_all | solution.py:53
  37.6 4.9 %stack.2 = bf16[8,16,56,768]{3,2,1,0:T(8,128)(2,1)} broadcast(bf16[16,56,768]{2,1,0:T(8,128)(2,1)S(1)} %all_to_all.20), dimensions={1,2,3} | broadcast | bytes 12386304 | tf_op jit(solution)/shard_map/stack | solution.py:56
  42.6 128.4 %all_to_all.21 = bf16[8,16,56,768]{3,2,1,0:T(8,128)(2,1)S(1)} all-to-all(bf16[8,16,56,768]{3,2,1,0:T(8,128)(2,1)} %stack.2), channel_id=1, replica_groups=mesh['seq'=16,'tp'=8] {'tp'}, dimensions={0} | all-to-all | bytes 22020096 | tf_op jit(solution)/shard_map/all_to_all | solution.py:56
  171.0 22.3 %copy.32 = bf16[16,56,8,768]{3,2,1,0:T(8,128)(2,1)S(1)} copy(bf16[16,56,8,768]{3,1,0,2:T(8,128)(2,1)S(1)} %bitcast.39) | data formatting | bytes 22020096 | tf_op jit(solution)/shard_map/reshape | solution.py:55
  193.3 3.2 %copy.35 = bf16[112,8,8,768]{3,1,2,0:T(8,128)(2,1)S(1)} copy(bf16[112,8,8,768]{3,2,1,0:T(8,128)(2,1)S(1)} %bitcast.40) | data formatting | bytes 22020096
  196.6 5.8 %fusion.3 = f32[896,512]{1,0:T(8,128)S(1)} fusion(bf16[896,6144]{1,0:T(8,128)(2,1)S(1)} %bitcast.42, bf16[1,6144,512]{2,1,0:T(8,128)(2,1)S(1)} %bitcast.48), kind=kOutput, calls=%fused_computation.5 | convolution fusion | flops 5637144576 | bytes 19136512 | tf_op jit(solution)/shard_map/dot_general | solution.py:59
  202.4 8.0 %multiply_convert_fusion = bf16[896,512]{1,0:T(8,128)(2,1)S(1)} fusion(f32[896,512]{1,0:T(8,128)S(1)} %fusion.3, bf16[896,6144]{1,0:T(8,128)(2,1)S(1)} %bitcast.43, bf16[1,6144,512]{2,1,0:T(8,128)(2,1)} %param.10), kind=kOutput, calls=%fused_computation.8 | convolution fusion | flops 5639897088 | bytes 20054016 | tf_op jit(solution)/shard_map/dot_general | solution.py:60
  210.5 11.3 %convolution_convert_fusion = bf16[16,56,6144]{2,1,0:T(8,128)(2,1)} fusion(bf16[16,56,512]{2,1,0:T(8,128)(2,1)S(1)} %bitcast.49, bf16[1,512,6144]{2,1,0:T(8,128)(2,1)} %param.11), kind=kOutput, calls=%fused_computation.1 | convolution fusion | flops 5642649600 | bytes 18219008 | tf_op jit(solution)/shard_map/dot_general | solution.py:62
  221.8 0.0 reduce-scatter.2.cloned.1.call-update
  221.8 0.7 copy-done.2
  222.5 0.1 fusion.19
  222.6 7.6 %all_to_all.22 = f32[8,128,8]{1,2,0:T(8,128)S(1)} all-to-all(f32[8,128,8]{1,2,0:T(8,128)S(1)} %broadcast_in_dim.10), channel_id=1, replica_groups=mesh['seq'=16,'tp'=8] {'tp'}, dimensions={0} | all-to-all | bytes 65536 | tf_op jit(solution)/shard_map/all_to_all | solution.py:12
  230.2 52.3 %reduce-scatter.2.cloned.1.call-done = bf16[16,56,768]{2,1,0:T(8,128)(2,1)} async-done(((bf16[16,56,6144]{2,1,0:T(8,128)(2,1)}), bf16[16,56,768]{2,1,0:T(8,128)(2,1)}) %reduce-scatter.2.cloned.1.call-update) | async-done | bytes 1376272 | tf_op jit(solution)/shard_map/reduce_scatter | solution.py:65
  282.6 6.6 %all-to-all-start.2 = ((bf16[16,56,768]{2,1,0:T(8,128)(2,1)}), bf16[16,56,768]{2,1,0:T(8,128)(2,1)S(1)}, u32[]{:S(2)}, u32[]{:S(2)}) async-start(bf16[16,56,768]{2,1,0:T(8,128)(2,1)} %reduce-scatter.2.cloned.1.call-done), calls=%async_computation.3 | async-start | bytes 2752512 | tf_op jit(solution)/shard_map/all_to_all | solution.py:68
  289.2 0.1 copy.33
  289.3 0.1 mul.39
  289.5 0.1 copy.34
  289.7 24.0 %all-to-all-done.2 = bf16[16,56,768]{2,1,0:T(8,128)(2,1)S(1)} async-done(((bf16[16,56,768]{2,1,0:T(8,128)(2,1)}), bf16[16,56,768]{2,1,0:T(8,128)(2,1)S(1)}, u32[]{:S(2)}, u32[]{:S(2)}) %all-to-all-start.2) | async-done | bytes 1376288 | tf_op jit(solution)/shard_map/all_to_all | solution.py:68
  313.6 0.2 convert_reduce_fusion
  313.9 1.1 gather_fusion
  315.0 0.5 reshape.135
  315.4 1.7 multiply_reduce_fusion
  (23 shorter events, 0.2 us)
Async XLA Ops:
  6.5 3.3 %copy-start = (bf16[128,768]{1,0:T(8,128)(2,1)S(1)}, bf16[128,768]{1,0:T(8,128)(2,1)}, u32[]{:S(2)}) copy-start(bf16[128,768]{1,0:T(8,128)(2,1)} %param.6) | copy-start | bytes 589828
  6.5 276.0 %reduce-scatter.2.cloned.1.call-start = ((), (), s32[]{:S(2)}) async-start(), calls=%async_computation.5 | async-start | bytes 12386304 | tf_op jit(solution)/shard_map/reduce_scatter | solution.py:65
  171.0 25.6 %slice-start = ((s8[6291456]{0:T(1024)(128)(4,1)}), s8[4194304]{0:T(1024)(128)(4,1)S(1)}, s32[]{:S(2)}) async-start(s8[6291456]{0:T(1024)(128)(4,1)} %bitcast.47), calls=%async_computation.6 | async-start | bytes 8388608
  193.3 3.3 %slice-start.1 = ((s8[6291456]{0:T(1024)(128)(4,1)}), s8[2097152]{0:T(1024)(128)(4,1)S(1)}, s32[]{:S(2)}) async-start(s8[6291456]{0:T(1024)(128)(4,1)} %bitcast.47), calls=%async_computation.7 | async-start | bytes 4194304
  221.8 0.7 copy-start.2
  221.8 67.4 %copy-start.1 = (s32[128,2]{0,1:T(2,128)S(1)}, s32[128,2]{0,1:T(2,128)}, u32[]{:S(2)}) copy-start(s32[128,2]{0,1:T(2,128)} %param.8) | copy-start | bytes 3076
  282.6 31.1 %all-to-all-start.2 = ((bf16[16,56,768]{2,1,0:T(8,128)(2,1)}), bf16[16,56,768]{2,1,0:T(8,128)(2,1)S(1)}, u32[]{:S(2)}, u32[]{:S(2)}) async-start(bf16[16,56,768]{2,1,0:T(8,128)(2,1)} %reduce-scatter.2.cloned.1.call-done), calls=%async_computation.3 | async-start | bytes 2752512 | tf_op jit(solution)/shard_map/all_to_all | solution.py:68
Sparse Core Ops, SparseCore 0:
  222.0 60.5 reduce-scatter.1
